TPU v7x, 32 devices: a whole 2x2x4 slice. The times are simulated.
32 devices in a mesh: ctx: 8 (over z, x), heads: 4 (over y, core).
Axes of the slice: x: 2, y: 2, z: 4, core: 2. Of those that a mesh axis runs over, the one named last changes fastest.
Arguments:
- query_rows: bfloat16 [8, 16, 2, 128], P('ctx', 'heads'), may hold values from -6 to 6
- past_keys: bfloat16 [8, 16, 512, 128], P(None, 'heads', 'ctx'), may hold values from -6 to 6
- past_values: bfloat16 [8, 16, 512, 128], P(None, 'heads', 'ctx'), may hold values from -6 to 6
- used_length: int32 [8], replicated, may hold values from 256 to 512
Outputs:
- read: bfloat16 [8, 16, 2, 128], P('ctx', 'heads')
All inputs are finite; a program needn't handle non-finite values.
Results may differ from a plain program's by a relative error of at most 0.0015.
Values may be sent and summed in bfloat16 or wider, within the bound.
A program may use at most 64 MiB of HBM per device.

v0:
```python
import jax
import jax.numpy as jnp
from jax import lax
from jax.sharding import PartitionSpec as P

HEAD_SIZE = 128


def local(query_rows, past_keys, past_values, used_length):
    all_queries = lax.all_gather(query_rows, "ctx", axis=0, tiled=True)
    logit = jnp.einsum(
        "bkgd,bktd->bkgt", all_queries, past_keys, preferred_element_type=jnp.float32
    ) * HEAD_SIZE ** (-0.5)
    positions = lax.axis_index("ctx") * past_keys.shape[2] + jnp.arange(past_keys.shape[2])
    filled = positions[None, :] < used_length[:, None]
    logit = jnp.where(filled[:, None, None, :], logit, -1e30)
    top = jnp.max(logit, axis=-1)
    part = jnp.where(filled[:, None, None, :], jnp.exp(logit - top[..., None]), 0.0)
    weight_sum = jnp.sum(part, axis=-1)
    read_sum = jnp.einsum(
        "bkgt,bktd->bkgd", part, past_values.astype(jnp.float32), precision=lax.Precision.HIGHEST
    )
    tops, sums, parts = (
        lax.all_to_all(top[None], "ctx", split_axis=1, concat_axis=0, tiled=True),
        lax.all_to_all(weight_sum[None], "ctx", split_axis=1, concat_axis=0, tiled=True),
        lax.all_to_all(read_sum[None], "ctx", split_axis=1, concat_axis=0, tiled=True),
    )
    best = jnp.max(tops, axis=0)
    scale = jnp.exp(tops - best)
    weight_own = jnp.sum(sums * scale, axis=0)
    read_own = jnp.sum(parts * scale[..., None], axis=0)
    read = (read_own / weight_own[..., None]).astype(jnp.bfloat16)
    return read


def solution(mesh):
    return jax.shard_map(
        local,
        mesh=mesh,
        in_specs=(
            P("ctx", "heads", None, None),
            P(None, "heads", "ctx", None),
            P(None, "heads", "ctx", None),
            P(),
        ),
        out_specs=P("ctx", "heads", None, None),
        check_vma=False,
    )
```

profile of v0, /device:TPU:0, one launch (start us, length us, event | category | flops | bytes accessed | tf_op | source)
XLA Modules:
  0.0 62.1 jit_solution(10074065572557208397)
XLA Ops:
  0.0 0.0 copy-start
  0.0 0.0 copy-start.1
  0.0 0.7 %copy-done.1 = bf16[1,4,2,128]{3,2,1,0:T(2,128)(2,1)S(1)} copy-done((bf16[1,4,2,128]{3,2,1,0:T(2,128)(2,1)S(1)}, bf16[1,4,2,128]{3,2,1,0:T(2,128)(2,1)}, u32[]{:S(2)}) %copy-start.1) | copy-done | bytes 2072
  0.7 0.0 copy-start.2
  0.8 28.1 %all_gather.3 = bf16[8,4,2,128]{3,1,2,0:T(4,128)(2,1)S(1)} all-gather(bf16[1,4,2,128]{3,1,2,0:T(4,128)(2,1)S(1)} %copy.7), channel_id=1, replica_groups=mesh['ctx'=8,'heads'=4] {'ctx'}, dimensions={0}, use_global_device_ids=true | all-gather | bytes 18432 | tf_op jit(solution)/shard_map/all_gather | solution.py:10
  28.8 0.0 copy-done.2
  28.8 0.1 broadcast_compare_fusion
  28.9 1.5 %fusion.10 = (f32[8,4,2]{2,1,0:T(4,128)S(1)}, f32[8,4,2,64]{3,2,1,0:T(2,128)S(1)}) fusion(bf16[8,4,64,128]{3,2,1,0:T(8,128)(2,1)} %param.5, bf16[8,4,2,128]{3,1,2,0:T(4,128)(2,1)S(1)} %all_gather.3, pred[8,64]{1,0:T(8,128)(4,1)S(1)} %broadcast_compare_fusion), kind=kOutput, calls=%fused_computation.19 | convolution fusion | flops 1060800 | bytes 557824 | tf_op jit(solution)/shard_map/bkgd,bktd->bkgt/dot_general | solution.py:11
  30.4 0.7 %copy.11 = f32[1,8,4,2]{2,3,0,1:T(2,128)} copy(f32[1,8,4,2]{3,2,1,0:T(4,128)S(1)} %bitcast.30) | data formatting | bytes 512 | tf_op jit(solution)/shard_map/broadcast_in_dim | solution.py:24
  31.1 4.0 %all-to-all-start.1 = ((f32[1,8,4,2]{2,3,0,1:T(2,128)}), f32[1,8,4,2]{2,3,0,1:T(2,128)S(1)}, u32[]{:S(2)}, u32[]{:S(2)}) async-start(f32[1,8,4,2]{2,3,0,1:T(2,128)} %copy.11), calls=%async_computation.1 | async-start | bytes 16384 | tf_op jit(solution)/shard_map/all_to_all | solution.py:24
  35.1 0.0 copy-done
  35.1 1.2 %convolution_bitcast_fusion = f32[1,8,4,2,128]{4,3,2,0,1:T(2,128)} fusion(bf16[8,4,64,128]{3,2,1,0:T(8,128)(2,1)S(1)} %copy-done, f32[8,4,2,64]{3,2,1,0:T(2,128)S(1)} %get-tuple-element.6, pred[8,64]{1,0:T(8,128)(4,1)S(1)} %broadcast_compare_fusion, f32[8,4,2]{2,1,0:T(4,128)S(1)} %get-tuple-element.5), kind=kOutput, calls=%fused_computation | convolution fusion | flops 6299648 | bytes 574208 | tf_op jit(solution)/shard_map/bkgt,bktd->bkgd/dot_general | solution.py:20
  36.3 0.2 fusion.8
  36.5 0.7 %copy.15 = f32[1,8,4,2]{2,3,0,1:T(2,128)} copy(f32[1,8,4,2]{3,2,1,0:T(4,128)S(1)} %bitcast.31) | data formatting | bytes 512 | tf_op jit(solution)/shard_map/broadcast_in_dim | solution.py:25
  37.2 4.4 %all-to-all-done.1 = f32[1,8,4,2]{2,3,0,1:T(2,128)S(1)} async-done(((f32[1,8,4,2]{2,3,0,1:T(2,128)}), f32[1,8,4,2]{2,3,0,1:T(2,128)S(1)}, u32[]{:S(2)}, u32[]{:S(2)}) %all-to-all-start.1) | async-done | bytes 288 | tf_op jit(solution)/shard_map/all_to_all | solution.py:24
  41.6 3.3 %all-to-all-start.2 = ((f32[1,8,4,2]{2,3,0,1:T(2,128)}), f32[1,8,4,2]{2,3,0,1:T(2,128)S(1)}, u32[]{:S(2)}, u32[]{:S(2)}) async-start(f32[1,8,4,2]{2,3,0,1:T(2,128)} %copy.15), calls=%async_computation.2 | async-start | bytes 16384 | tf_op jit(solution)/shard_map/all_to_all | solution.py:25
  44.9 0.1 copy.12
  45.0 0.1 fusion.6
  45.1 6.3 %all-to-all-done.2 = f32[1,8,4,2]{2,3,0,1:T(2,128)S(1)} async-done(((f32[1,8,4,2]{2,3,0,1:T(2,128)}), f32[1,8,4,2]{2,3,0,1:T(2,128)S(1)}, u32[]{:S(2)}, u32[]{:S(2)}) %all-to-all-start.2) | async-done | bytes 288 | tf_op jit(solution)/shard_map/all_to_all | solution.py:25
  51.4 3.3 %all-to-all-start = ((f32[1,8,4,2,128]{4,3,2,0,1:T(2,128)}), f32[1,8,4,2,128]{4,3,2,0,1:T(2,128)S(1)}, u32[]{:S(2)}, u32[]{:S(2)}) async-start(f32[1,8,4,2,128]{4,3,2,0,1:T(2,128)} %convolution_bitcast_fusion), calls=%async_computation | async-start | bytes 65536 | tf_op jit(solution)/shard_map/all_to_all | solution.py:26
  54.7 0.1 copy.16
  54.8 0.2 fusion.5
  55.0 0.1 copy.18
  55.1 0.1 copy.13
  55.2 6.2 %all-to-all-done = f32[1,8,4,2,128]{4,3,2,0,1:T(2,128)S(1)} async-done(((f32[1,8,4,2,128]{4,3,2,0,1:T(2,128)}), f32[1,8,4,2,128]{4,3,2,0,1:T(2,128)S(1)}, u32[]{:S(2)}, u32[]{:S(2)}) %all-to-all-start) | async-done | bytes 32800 | tf_op jit(solution)/shard_map/all_to_all | solution.py:26
  61.4 0.1 fusion.1
  61.5 0.7 %fusion.7 = bf16[1,4,2,128]{3,2,1,0:T(2,128)(2,1)} fusion(f32[4,2,128]{2,1,0:T(2,128)S(1)} %fusion.1, f32[4,2]{1,0:T(4,128)S(1)} %copy.18), kind=kLoop, calls=%fused_computation.14 | loop fusion | flops 2048 | bytes 6176 | tf_op jit(solution)/shard_map/convert_element_type | solution.py:32
  (3 shorter events, 0.0 us)
Async XLA Ops:
  0.0 35.1 %copy-start = (bf16[8,4,64,128]{3,2,1,0:T(8,128)(2,1)S(1)}, bf16[8,4,64,128]{3,2,1,0:T(8,128)(2,1)}, u32[]{:S(2)}) copy-start(bf16[8,4,64,128]{3,2,1,0:T(8,128)(2,1)} %param.6) | copy-start | bytes 1572868
  0.0 0.7 %copy-start.1 = (bf16[1,4,2,128]{3,2,1,0:T(2,128)(2,1)S(1)}, bf16[1,4,2,128]{3,2,1,0:T(2,128)(2,1)}, u32[]{:S(2)}) copy-start(bf16[1,4,2,128]{3,2,1,0:T(2,128)(2,1)} %param.4) | copy-start | bytes 6148
  0.7 28.1 %copy-start.2 = (s32[8]{0:T(128)S(1)}, s32[8]{0:T(128)}, u32[]{:S(2)}) copy-start(s32[8]{0:T(128)} %param.7) | copy-start | bytes 100
  31.1 10.5 %all-to-all-start.1 = ((f32[1,8,4,2]{2,3,0,1:T(2,128)}), f32[1,8,4,2]{2,3,0,1:T(2,128)S(1)}, u32[]{:S(2)}, u32[]{:S(2)}) async-start(f32[1,8,4,2]{2,3,0,1:T(2,128)} %copy.11), calls=%async_computation.1 | async-start | bytes 16384 | tf_op jit(solution)/shard_map/all_to_all | solution.py:24
  41.6 9.8 %all-to-all-start.2 = ((f32[1,8,4,2]{2,3,0,1:T(2,128)}), f32[1,8,4,2]{2,3,0,1:T(2,128)S(1)}, u32[]{:S(2)}, u32[]{:S(2)}) async-start(f32[1,8,4,2]{2,3,0,1:T(2,128)} %copy.15), calls=%async_computation.2 | async-start | bytes 16384 | tf_op jit(solution)/shard_map/all_to_all | solution.py:25
  51.4 10.0 %all-to-all-start = ((f32[1,8,4,2,128]{4,3,2,0,1:T(2,128)}), f32[1,8,4,2,128]{4,3,2,0,1:T(2,128)S(1)}, u32[]{:S(2)}, u32[]{:S(2)}) async-start(f32[1,8,4,2,128]{4,3,2,0,1:T(2,128)} %convolution_bitcast_fusion), calls=%async_computation | async-start | bytes 65536 | tf_op jit(solution)/shard_map/all_to_all | solution.py:26
where the time goes:
time: 62.5 us; the launch traced here: 62.1 us
  blocking collectives  28.1 us (45%)
  waiting for transfers between devices  16.8 us (27%)
  starting transfers between devices  10.6 us (17%)
  matrix products  2.71 us (4%)
  local copies, waits for them, and re-layouts  2.59 us (4%)
  other arithmetic  1.32 us (2%)
    all_gather x1, blocking collectives, local(): all_queries = lax.all_gather(query_rows, 'ctx', axis=0, tiled=True)  28.1 us
    all_to_all x1, waiting for transfers between devices, local(): lax.all_to_all(weight_sum[None], 'ctx', split_axis=1, concat_axis=0, tile...  6.27 us
    all_to_all x1, waiting for transfers between devices, local(): lax.all_to_all(read_sum[None], 'ctx', split_axis=1, concat_axis=0, tiled=...  6.17 us
    all_to_all x1, waiting for transfers between devices, local(): lax.all_to_all(top[None], 'ctx', split_axis=1, concat_axis=0, tiled=True)  4.37 us
    all_to_all x1, starting transfers between devices, local(): lax.all_to_all(top[None], 'ctx', split_axis=1, concat_axis=0, tiled=True)  3.97 us
    all_to_all x1, starting transfers between devices, local(): lax.all_to_all(read_sum[None], 'ctx', split_axis=1, concat_axis=0, tiled=...  3.33 us
    all_to_all x1, starting transfers between devices, local(): lax.all_to_all(weight_sum[None], 'ctx', split_axis=1, concat_axis=0, tile...  3.32 us
    dot_general x1, matrix products, local(): jnp.einsum('bkgd,bktd->bkgt', all_queries, past_keys, preferred_element_t...  1.51 us
  transfers between devices with their start and end apart: 3, of which 3 were waited for; matrix products, arithmetic and copies ran while one was open for 4% of the time, Pallas kernels for 0%

commit v1 on v0

--- a/solution.py
+++ b/solution.py
@@ -6,8 +6,30 @@
 HEAD_SIZE = 128
 
 
+def laid_out(tiles, dim):
+    tiles = jnp.moveaxis(tiles, 0, dim)
+    shape = tiles.shape
+    return tiles.reshape(*shape[:dim], shape[dim] * shape[dim + 1], *shape[dim + 2 :])
+
+
+def collected_by_bits(shard, axis):
+    size = lax.axis_size(axis)
+    pieces = shard[None]
+    for level in range(size.bit_length() - 1):
+        distance = 1 << level
+        partner_block = lax.ppermute(pieces, axis, [(i, i ^ distance) for i in range(size)])
+        both = jnp.stack([pieces, partner_block])
+        upper = lax.axis_index(axis) >> level & 1
+        pieces = jnp.where(upper == 0, both, both[::-1]).reshape(-1, *shard.shape)
+    return pieces
+
+
+def doubled_up(x, axis, dim):
+    return laid_out(collected_by_bits(x, axis), dim)
+
+
 def local(query_rows, past_keys, past_values, used_length):
-    all_queries = lax.all_gather(query_rows, "ctx", axis=0, tiled=True)
+    all_queries = doubled_up(query_rows, "ctx", 0)
     logit = jnp.einsum(
         "bkgd,bktd->bkgt", all_queries, past_keys, preferred_element_type=jnp.float32
     ) * HEAD_SIZE ** (-0.5)

time: 62.5 us -> 49.1 us (0.79)
  blocking collectives: 28.1 us -> 0 us
  starting transfers between devices: 10.6 us -> 21 us
  waiting for transfers between devices: 16.8 us -> 21.7 us
  local copies, waits for them, and re-layouts: 2.59 us -> 1.86 us
    all_gather x1 -> x0, blocking collectives: 28.1 us -> none  [local(): all_queries = lax.all_gather(query_rows, 'ctx', axis=0, tiled=True)]
    ppermute x0 -> x3, starting transfers between devices: none -> 8.24 us  [collected_by_bits(): lax.ppermute(pieces, axis, [(i, i ^ distance) for i in range(size)])]
    ppermute x0 -> x3, waiting for transfers between devices: none -> 4.91 us  [collected_by_bits(): lax.ppermute(pieces, axis, [(i, i ^ distance) for i in range(size)])]
    all_to_all x1, starting transfers between devices: 3.97 us -> 6.14 us  [local(): lax.all_to_all(top[None], 'ctx', split_axis=1, concat_axis=0, tiled=True)]
    unnamed x7 -> x6, local copies, waits for them, and re-layouts: 0.75 us -> 0.01 us
  transfers between devices with their start and end apart: 3 -> 6, of which waited for: 3 -> 6; matrix products, arithmetic and copies ran while one was open for 4% -> 6% of each run, Pallas kernels for 0% -> 0%
where the time goes in v1:
time: 49.1 us; the launch traced here: 48.8 us
  waiting for transfers between devices  21.7 us (44%)
  starting transfers between devices  21 us (43%)
  matrix products  2.7 us (5%)
  local copies, waits for them, and re-layouts  1.86 us (4%)
  other arithmetic  1.41 us (3%)
    ppermute x3, starting transfers between devices, collected_by_bits(): lax.ppermute(pieces, axis, [(i, i ^ distance) for i in range(size)])  8.24 us
    all_to_all x1, waiting for transfers between devices, local(): lax.all_to_all(weight_sum[None], 'ctx', split_axis=1, concat_axis=0, tile...  6.27 us
    all_to_all x1, waiting for transfers between devices, local(): lax.all_to_all(read_sum[None], 'ctx', split_axis=1, concat_axis=0, tiled=...  6.17 us
    all_to_all x1, starting transfers between devices, local(): lax.all_to_all(top[None], 'ctx', split_axis=1, concat_axis=0, tiled=True)  6.14 us
    ppermute x3, waiting for transfers between devices, collected_by_bits(): lax.ppermute(pieces, axis, [(i, i ^ distance) for i in range(size)])  4.91 us
    all_to_all x1, waiting for transfers between devices, local(): lax.all_to_all(top[None], 'ctx', split_axis=1, concat_axis=0, tiled=True)  4.37 us
    all_to_all x1, starting transfers between devices, local(): lax.all_to_all(read_sum[None], 'ctx', split_axis=1, concat_axis=0, tiled=...  3.33 us
    all_to_all x1, starting transfers between devices, local(): lax.all_to_all(weight_sum[None], 'ctx', split_axis=1, concat_axis=0, tile...  3.32 us
  transfers between devices with their start and end apart: 6, of which 6 were waited for; matrix products, arithmetic and copies ran while one was open for 6% of the time, Pallas kernels for 0%

profile of v1, /device:TPU:0, one launch (start us, length us, event | category | flops | bytes accessed | tf_op | source)
XLA Modules:
  0.0 48.8 jit_solution(54542594378320308)
XLA Ops:
  0.0 0.0 copy-start
  0.0 3.0 %collective-permute-start = (bf16[1,1,4,2,128]{4,3,2,1,0:T(2,128)(2,1)}, bf16[1,1,4,2,128]{4,3,2,1,0:T(2,128)(2,1)S(1)}, u32[]{:S(2)}, u32[]{:S(2)}) collective-permute-start(bf16[1,1,4,2,128]{4,3,2,1,0:T(2,128)(2,1)} %bitcast.50), channel_id=1, source_target_pairs={{0,4},{4,0},{8,12},{12,8},{16,20},{20,16},{24,28},{28,24},{1,5},{5... | collective-permute-start | bytes 6152 | tf_op jit(solution)/shard_map/ppermute | solution.py:20
  3.0 0.0 copy-start.1
  3.0 1.8 %collective-permute-done = bf16[1,1,4,2,128]{4,3,2,1,0:T(2,128)(2,1)S(1)} collective-permute-done((bf16[1,1,4,2,128]{4,3,2,1,0:T(2,128)(2,1)}, bf16[1,1,4,2,128]{4,3,2,1,0:T(2,128)(2,1)S(1)}, u32[]{:S(2)}, u32[]{:S(2)}) %collective-permute-start) | collective-permute-done | bytes 2080 | tf_op jit(solution)/shard_map/ppermute | solution.py:20
  4.7 0.0 copy-done.1
  4.8 2.2 %collective-permute-start.1 = (bf16[2,1,4,2,128]{4,3,2,0,1:T(2,128)(2,1)S(1)}, bf16[2,1,4,2,128]{4,3,2,0,1:T(2,128)(2,1)S(1)}, u32[]{:S(2)}, u32[]{:S(2)}) collective-permute-start(bf16[2,1,4,2,128]{4,3,2,0,1:T(2,128)(2,1)S(1)} %get-tuple-element.6), channel_id=1, source_target_pairs={{0,8},{4,12},{8,0},{12,4},{16,24},{20,28},{24,16},{28,20},{1,9},{5... | collective-permute-start | bytes 12296 | tf_op jit(solution)/shard_map/ppermute | solution.py:20
  7.0 1.6 %collective-permute-done.1 = bf16[2,1,4,2,128]{4,3,2,0,1:T(2,128)(2,1)S(1)} collective-permute-done((bf16[2,1,4,2,128]{4,3,2,0,1:T(2,128)(2,1)S(1)}, bf16[2,1,4,2,128]{4,3,2,0,1:T(2,128)(2,1)S(1)}, u32[]{:S(2)}, u32[]{:S(2)}) %collective-permute-start.1) | collective-permute-done | bytes 4128 | tf_op jit(solution)/shard_map/ppermute | solution.py:20
  8.6 0.0 copy-start.2
  8.6 3.1 %collective-permute-start.2 = (bf16[4,1,4,2,128]{4,3,2,0,1:T(2,128)(2,1)S(1)}, bf16[4,1,4,2,128]{4,3,2,0,1:T(2,128)(2,1)S(1)}, u32[]{:S(2)}, u32[]{:S(2)}) collective-permute-start(bf16[4,1,4,2,128]{4,3,2,0,1:T(2,128)(2,1)S(1)} %bitcast.46), channel_id=1, source_target_pairs={{0,16},{4,20},{8,24},{12,28},{16,0},{20,4},{24,8},{28,12},{1,17},{... | collective-permute-start | bytes 24584 | tf_op jit(solution)/shard_map/ppermute | solution.py:20
  11.7 0.0 copy-done.2
  11.7 0.1 broadcast_compare_fusion
  11.8 1.6 %collective-permute-done.2 = bf16[4,1,4,2,128]{4,3,2,0,1:T(2,128)(2,1)S(1)} collective-permute-done((bf16[4,1,4,2,128]{4,3,2,0,1:T(2,128)(2,1)S(1)}, bf16[4,1,4,2,128]{4,3,2,0,1:T(2,128)(2,1)S(1)}, u32[]{:S(2)}, u32[]{:S(2)}) %collective-permute-start.2) | collective-permute-done | bytes 8224 | tf_op jit(solution)/shard_map/ppermute | solution.py:20
  13.4 1.5 %fusion.11 = (f32[8,4,2]{2,1,0:T(4,128)S(1)}, f32[8,4,2,64]{3,2,1,0:T(2,128)S(1)}) fusion(bf16[8,4,2,128]{3,2,1,0:T(2,128)(2,1)S(1)} %bitcast.44, bf16[8,4,64,128]{3,2,1,0:T(8,128)(2,1)} %param.5, pred[8,64]{1,0:T(8,128)(4,1)S(1)} %broadcast_compare_fusion), kind=kOutput, calls=%fused_computation.26 | convolution fusion | flops 1060800 | bytes 557824 | tf_op jit(solution)/shard_map/bkgd,bktd->bkgt/dot_general | solution.py:33
  14.9 0.7 %copy.9 = f32[1,8,4,2]{2,3,0,1:T(2,128)} copy(f32[1,8,4,2]{3,2,1,0:T(4,128)S(1)} %bitcast.43) | data formatting | bytes 512 | tf_op jit(solution)/shard_map/broadcast_in_dim | solution.py:46
  15.6 6.1 %all-to-all-start.1 = ((f32[1,8,4,2]{2,3,0,1:T(2,128)}), f32[1,8,4,2]{2,3,0,1:T(2,128)S(1)}, u32[]{:S(2)}, u32[]{:S(2)}) async-start(f32[1,8,4,2]{2,3,0,1:T(2,128)} %copy.9), calls=%async_computation.1 | async-start | bytes 16384 | tf_op jit(solution)/shard_map/all_to_all | solution.py:46
  21.8 0.0 copy-done
  21.8 1.2 %convolution_bitcast_fusion = f32[1,8,4,2,128]{4,3,2,0,1:T(2,128)} fusion(bf16[8,4,64,128]{3,2,1,0:T(8,128)(2,1)S(1)} %copy-done, f32[8,4,2,64]{3,2,1,0:T(2,128)S(1)} %get-tuple-element.8, pred[8,64]{1,0:T(8,128)(4,1)S(1)} %broadcast_compare_fusion, f32[8,4,2]{2,1,0:T(4,128)S(1)} %get-tuple-element.7), kind=kOutput, calls=%fused_computation | convolution fusion | flops 6299648 | bytes 574208 | tf_op jit(solution)/shard_map/bkgt,bktd->bkgd/dot_general | solution.py:42
  23.0 0.2 fusion.7
  23.2 0.7 %copy.13 = f32[1,8,4,2]{2,3,0,1:T(2,128)} copy(f32[1,8,4,2]{3,2,1,0:T(4,128)S(1)} %bitcast.45) | data formatting | bytes 512 | tf_op jit(solution)/shard_map/broadcast_in_dim | solution.py:47
  23.9 4.4 %all-to-all-done.1 = f32[1,8,4,2]{2,3,0,1:T(2,128)S(1)} async-done(((f32[1,8,4,2]{2,3,0,1:T(2,128)}), f32[1,8,4,2]{2,3,0,1:T(2,128)S(1)}, u32[]{:S(2)}, u32[]{:S(2)}) %all-to-all-start.1) | async-done | bytes 288 | tf_op jit(solution)/shard_map/all_to_all | solution.py:46
  28.3 3.3 %all-to-all-start.2 = ((f32[1,8,4,2]{2,3,0,1:T(2,128)}), f32[1,8,4,2]{2,3,0,1:T(2,128)S(1)}, u32[]{:S(2)}, u32[]{:S(2)}) async-start(f32[1,8,4,2]{2,3,0,1:T(2,128)} %copy.13), calls=%async_computation.2 | async-start | bytes 16384 | tf_op jit(solution)/shard_map/all_to_all | solution.py:47
  31.6 0.1 copy.10
  31.7 0.1 fusion.5
  31.8 6.3 %all-to-all-done.2 = f32[1,8,4,2]{2,3,0,1:T(2,128)S(1)} async-done(((f32[1,8,4,2]{2,3,0,1:T(2,128)}), f32[1,8,4,2]{2,3,0,1:T(2,128)S(1)}, u32[]{:S(2)}, u32[]{:S(2)}) %all-to-all-start.2) | async-done | bytes 288 | tf_op jit(solution)/shard_map/all_to_all | solution.py:47
  38.1 3.3 %all-to-all-start = ((f32[1,8,4,2,128]{4,3,2,0,1:T(2,128)}), f32[1,8,4,2,128]{4,3,2,0,1:T(2,128)S(1)}, u32[]{:S(2)}, u32[]{:S(2)}) async-start(f32[1,8,4,2,128]{4,3,2,0,1:T(2,128)} %convolution_bitcast_fusion), calls=%async_computation | async-start | bytes 65536 | tf_op jit(solution)/shard_map/all_to_all | solution.py:48
  41.4 0.1 copy.14
  41.5 0.2 fusion.4
  41.7 0.1 copy.16
  41.8 0.1 copy.11
  41.9 6.2 %all-to-all-done = f32[1,8,4,2,128]{4,3,2,0,1:T(2,128)S(1)} async-done(((f32[1,8,4,2,128]{4,3,2,0,1:T(2,128)}), f32[1,8,4,2,128]{4,3,2,0,1:T(2,128)S(1)}, u32[]{:S(2)}, u32[]{:S(2)}) %all-to-all-start) | async-done | bytes 32800 | tf_op jit(solution)/shard_map/all_to_all | solution.py:48
  48.0 0.1 fusion.1
  48.1 0.7 %fusion.6 = bf16[1,4,2,128]{3,2,1,0:T(2,128)(2,1)} fusion(f32[4,2,128]{2,1,0:T(2,128)S(1)} %fusion.1, f32[4,2]{1,0:T(4,128)S(1)} %copy.16), kind=kLoop, calls=%fused_computation.19 | loop fusion | flops 2048 | bytes 6176 | tf_op jit(solution)/shard_map/convert_element_type | solution.py:54
  (8 shorter events, 0.1 us)
Async XLA Ops:
  0.0 21.8 %copy-start = (bf16[8,4,64,128]{3,2,1,0:T(8,128)(2,1)S(1)}, bf16[8,4,64,128]{3,2,1,0:T(8,128)(2,1)}, u32[]{:S(2)}) copy-start(bf16[8,4,64,128]{3,2,1,0:T(8,128)(2,1)} %param.6) | copy-start | bytes 1572868
  0.0 4.7 %collective-permute-start = (bf16[1,1,4,2,128]{4,3,2,1,0:T(2,128)(2,1)}, bf16[1,1,4,2,128]{4,3,2,1,0:T(2,128)(2,1)S(1)}, u32[]{:S(2)}, u32[]{:S(2)}) collective-permute-start(bf16[1,1,4,2,128]{4,3,2,1,0:T(2,128)(2,1)} %bitcast.50), channel_id=1, source_target_pairs={{0,4},{4,0},{8,12},{12,8},{16,20},{20,16},{24,28},{28,24},{1,5},{5... | collective-permute-start | bytes 6152 | tf_op jit(solution)/shard_map/ppermute | solution.py:20
  3.0 1.8 %copy-start.1 = (bf16[1,4,2,128]{3,2,1,0:T(2,128)(2,1)S(1)}, bf16[1,4,2,128]{3,2,1,0:T(2,128)(2,1)}, u32[]{:S(2)}) copy-start(bf16[1,4,2,128]{3,2,1,0:T(2,128)(2,1)} %param.4) | copy-start | bytes 6148
  4.8 3.8 %collective-permute-start.1 = (bf16[2,1,4,2,128]{4,3,2,0,1:T(2,128)(2,1)S(1)}, bf16[2,1,4,2,128]{4,3,2,0,1:T(2,128)(2,1)S(1)}, u32[]{:S(2)}, u32[]{:S(2)}) collective-permute-start(bf16[2,1,4,2,128]{4,3,2,0,1:T(2,128)(2,1)S(1)} %get-tuple-element.6), channel_id=1, source_target_pairs={{0,8},{4,12},{8,0},{12,4},{16,24},{20,28},{24,16},{28,20},{1,9},{5... | collective-permute-start | bytes 12296 | tf_op jit(solution)/shard_map/ppermute | solution.py:20
  8.6 3.1 %copy-start.2 = (s32[8]{0:T(128)S(1)}, s32[8]{0:T(128)}, u32[]{:S(2)}) copy-start(s32[8]{0:T(128)} %param.7) | copy-start | bytes 100
  8.6 4.7 %collective-permute-start.2 = (bf16[4,1,4,2,128]{4,3,2,0,1:T(2,128)(2,1)S(1)}, bf16[4,1,4,2,128]{4,3,2,0,1:T(2,128)(2,1)S(1)}, u32[]{:S(2)}, u32[]{:S(2)}) collective-permute-start(bf16[4,1,4,2,128]{4,3,2,0,1:T(2,128)(2,1)S(1)} %bitcast.46), channel_id=1, source_target_pairs={{0,16},{4,20},{8,24},{12,28},{16,0},{20,4},{24,8},{28,12},{1,17},{... | collective-permute-start | bytes 24584 | tf_op jit(solution)/shard_map/ppermute | solution.py:20
  15.6 12.7 %all-to-all-start.1 = ((f32[1,8,4,2]{2,3,0,1:T(2,128)}), f32[1,8,4,2]{2,3,0,1:T(2,128)S(1)}, u32[]{:S(2)}, u32[]{:S(2)}) async-start(f32[1,8,4,2]{2,3,0,1:T(2,128)} %copy.9), calls=%async_computation.1 | async-start | bytes 16384 | tf_op jit(solution)/shard_map/all_to_all | solution.py:46
  28.3 9.8 %all-to-all-start.2 = ((f32[1,8,4,2]{2,3,0,1:T(2,128)}), f32[1,8,4,2]{2,3,0,1:T(2,128)S(1)}, u32[]{:S(2)}, u32[]{:S(2)}) async-start(f32[1,8,4,2]{2,3,0,1:T(2,128)} %copy.13), calls=%async_computation.2 | async-start | bytes 16384 | tf_op jit(solution)/shard_map/all_to_all | solution.py:47
  38.1 10.0 %all-to-all-start = ((f32[1,8,4,2,128]{4,3,2,0,1:T(2,128)}), f32[1,8,4,2,128]{4,3,2,0,1:T(2,128)S(1)}, u32[]{:S(2)}, u32[]{:S(2)}) async-start(f32[1,8,4,2,128]{4,3,2,0,1:T(2,128)} %convolution_bitcast_fusion), calls=%async_computation | async-start | bytes 65536 | tf_op jit(solution)/shard_map/all_to_all | solution.py:48
